TPU v7x, 32 devices: a whole 2x2x4 slice. The times are simulated.
32 devices in a mesh: head: 4 (over x, core), seq: 8 (over z, y).
Axes of the slice: x: 2, y: 2, z: 4, core: 2. Of those that a mesh axis runs over, the one named last changes fastest.
Arguments:
- query: float32 [4096, 2048], P(('seq', 'head')), may hold values from -8 to 8
- key_in: float32 [4096, 1024], P(('seq', 'head')), may hold values from -8 to 8
- value_in: float32 [4096, 1024], P(('seq', 'head')), may hold values from -6 to 6
- d_out: float32 [4096, 2048], P(('seq', 'head')), may hold values from -48 to 48
Outputs:
- grad_query: float32 [4096, 2048], P(('seq', 'head'))
- grad_key: float32 [4096, 1024], P(('seq', 'head'))
- grad_value: float32 [4096, 1024], P(('seq', 'head'))
All inputs are finite; a program needn't handle non-finite values.
Results may differ from a plain program's by a relative error of at most 0.00045.
Values sent between devices are 32-bit elements; how exact they have to be, the bound alone decides.
No kernel may reach another device: no remote copies, remote signals or barrier semaphores. Data moves between devices by JAX's collectives and lax.ppermute only.
A program may use at most 64 MiB of HBM per device.

v0:
```python
import functools
import math

import jax
import jax.numpy as jnp
from jax import lax
from jax.experimental import pallas as pl
from jax.experimental.pallas import tpu as pltpu
from jax.sharding import PartitionSpec as P


HD = 128
WINDOW = 1024
KC = 128

score_scale = 168.0 ** (-0.5)
LOG2E = 1.0 / math.log(2.0)
f32 = jnp.float32
bf16 = jnp.bfloat16
BIG = 3.0e38
ATTN_VMEM = 36 << 20
MOVE_VMEM = 10 << 20


def split(x):
    hi = x.astype(bf16)
    lo = (x - hi.astype(f32)).astype(bf16)
    return hi, lo


def dot(a, b):
    return jnp.dot(a, b, preferred_element_type=f32)


def fold8(x, op):
    rows, cols = x.shape
    return op(x.reshape(rows // 8, 8, cols), axis=0)


QB = 128
KC = 64


def attn_kernel(
    group, stage, parts, carried, place_ref, *refs,
):
    blocks, refs = refs[:parts], refs[parts:]
    own, refs = refs[:parts], refs[parts:]
    near, rest, refs = refs[0], refs[1], refs[2:]
    given, refs = refs[:carried], refs[carried:]
    dq_ref, refs = refs[0], refs[1:]
    grads, refs = refs[:3], refs[3:]
    kaug, vaug, kt, dkacc, dvacc, sref, dpref = refs[:7]
    bufs, qbuf = refs[7:-1], refs[-1]
    me = place_ref[1]
    u = pl.program_id(0)
    steps = pl.num_programs(0)
    tokens = parts * QB
    half = tokens // 2
    done_rows = stage * half
    span = tokens + QB
    far_tiles = parts - stage * (parts // 2)
    lanes = group * QB
    sets = (bufs[:6], bufs[6:])
    first = place_ref[0] == 0

    @pl.when(u == 0)
    def _():
        count = parts // 2
        same = (me < count) == (stage == 0)

        def far_block(k):
            return near[k] if k < near.shape[0] else rest[k - near.shape[0]]

        def own_block(k):
            return own[k][...]

        def place_keys(kv, r):
            r = pl.multiple_of(r, QB)
            k = kv[:, :HD]
            hi, lo = split(k)
            kaug[pl.ds(r, QB), :HD] = hi
            kaug[pl.ds(r, QB), HD:] = lo
            vh, vl = split(kv[:, HD:])
            vaug[pl.ds(r, QB), :HD] = vh
            vaug[pl.ds(r, QB), HD:] = vl
            th, tl = split(k.T)
            kt[:HD, pl.ds(r, QB)] = th
            kt[HD:, pl.ds(r, QB)] = tl

        full, part = (far_block, own_block) if stage == 0 else (own_block, far_block)
        full_base, part_base = (0, tokens) if stage == 0 else (half, 0)
        for k in range(parts):
            place_keys(full(k), full_base + (me ^ k) * QB)
        for j in range(count):
            slot = (me ^ j) & (count - 1)
            place_keys(jnp.where(same, part(j), part(count + j)), part_base + slot * QB)
            qbuf[slot] = jnp.where(same, blocks[j][...], blocks[count + j][...])
        dkacc[...] = jnp.zeros_like(dkacc)
        dvacc[...] = jnp.zeros_like(dvacc)
        for buf in sets[1]:
            buf[...] = jnp.zeros_like(buf)
        if done_rows:
            dq_ref[:done_rows, :] = given[-1][...]

    rows = lax.broadcasted_iota(jnp.int32, (KC, lanes), 0)
    cols = lax.rem(lax.broadcasted_iota(jnp.int32, (KC, lanes), 1), QB)

    def products(tile, buf):
        phi, plo, dshi, dslo, qq, oo = buf
        a = pl.multiple_of(jnp.maximum(tile, 0) * QB, QB)
        q2 = qq[...]
        o2 = oo[...]
        for c in range(0, span, 192):
            dvacc[pl.ds(a + c, 192), :] += dot(phi[c:c + 192, :], o2) + dot(plo[c:c + 192, :], o2)
        for c in range(0, span, 192):
            dkacc[pl.ds(a + c, 192), :] += dot(dshi[c:c + 192, :], q2) + dot(dslo[c:c + 192, :], q2)
        kts = kt[:, pl.ds(a, span)]
        full = dot(kts, dshi[...]) + dot(kts, dslo[...])
        dqt = (full[:HD] + full[HD:]) * score_scale
        for h in range(group):
            dq_ref[pl.ds(done_rows + a, QB), h * HD:(h + 1) * HD] = dqt[:, h * QB:(h + 1) * QB].T

    def weights(tile, buf):
        slot = tile
        phi, plo, dshi, dslo, qq, oo = buf
        a = pl.multiple_of(tile * QB, QB)
        qts = []
        ots = []
        for h in range(group):
            q = qbuf[slot, :, h * HD:(h + 1) * HD] * (score_scale * LOG2E)
            o = qbuf[slot, :, (group + h) * HD:(group + h + 1) * HD]
            qh, ql = split(q)
            oh, ol = split(o)
            qq[h * QB:(h + 1) * QB, :HD] = qh
            qq[h * QB:(h + 1) * QB, HD:] = ql
            oo[h * QB:(h + 1) * QB, :HD] = oh
            oo[h * QB:(h + 1) * QB, HD:] = ol
            qts.append(q.T)
            ots.append(o.T)
        qth, qtl = split(jnp.concatenate(qts, axis=1))
        oth, otl = split(jnp.concatenate(ots, axis=1))
        qhh = jnp.concatenate([qth, qth], axis=0)
        qll = jnp.concatenate([qtl, qtl], axis=0)
        ohh = jnp.concatenate([oth, oth], axis=0)
        oll = jnp.concatenate([otl, otl], axis=0)
        for c in range(0, span, 192):
            ka = kaug[pl.ds(a + c, 192), :]
            sref[c:c + 192, :] = dot(ka, qhh) + dot(ka, qll)
        for c in range(0, span, 192):
            va = vaug[pl.ds(a + c, 192), :]
            dpref[c:c + 192, :] = dot(va, ohh) + dot(va, oll)

        def masked(c):
            s = sref[c:c + KC, :]
            if c < QB:
                s = jnp.where(rows + c > cols, s, -jnp.inf)
            elif c >= tokens:
                s = jnp.where(rows + (c - tokens) <= cols, s, -jnp.inf)
            return s

        def is_far(c):
            return jnp.logical_and(first, tile + c // QB < far_tiles)

        top = jnp.full((8, lanes), -jnp.inf, f32)
        for b in range(0, span, QB):
            part = jnp.full((8, lanes), -jnp.inf, f32)
            for c in range(b, b + QB, KC):
                part = jnp.maximum(part, fold8(masked(c), jnp.max))
            top = jnp.maximum(top, jnp.where(is_far(b), -jnp.inf, part))
        m = jnp.max(top, axis=0, keepdims=True)
        total = jnp.zeros((8, lanes), f32)
        dots = jnp.zeros((8, lanes), f32)
        for c in range(0, span, KC):
            shift = jnp.where(is_far(c), BIG, m)
            p = jnp.exp2(masked(c) - shift)
            total = total + fold8(p, jnp.sum)
            dots = dots + fold8(p * dpref[c:c + KC, :], jnp.sum)
            sref[c:c + KC, :] = p
        inv = 1.0 / jnp.sum(total, axis=0, keepdims=True)
        rd = jnp.sum(dots, axis=0, keepdims=True) * inv
        for c in range(0, span, KC):
            p = sref[c:c + KC, :] * inv
            ds = p * (dpref[c:c + KC, :] - rd)
            hi, lo = split(p)
            phi[c:c + KC, :] = hi
            plo[c:c + KC, :] = lo
            hi, lo = split(ds)
            dshi[c:c + KC, :] = hi
            dslo[c:c + KC, :] = lo

    for n in range(2):
        tile = 2 * u + n
        products(tile - 1, sets[1 - n])
        weights(tile, sets[n])

    @pl.when(u == steps - 1)
    def _():
        products(2 * u + 1, sets[1])
        for n, ref in enumerate(grads):
            base = n * half
            for r in range(0, half, QB):
                dk = dkacc[pl.ds(base + r, QB), :]
                dv = dvacc[pl.ds(base + r, QB), :]
                dk = (dk[:, :HD] + dk[:, HD:]) * (1.0 / LOG2E)
                dv = dv[:, :HD] + dv[:, HD:]
                if n < carried - 1:
                    dk = dk + given[n][pl.ds(r, QB), :HD]
                    dv = dv + given[n][pl.ds(r, QB), HD:]
                ref[pl.ds(r, QB), :HD] = dk
                ref[pl.ds(r, QB), HD:] = dv


def attn(place, blocks, part, far, own, given, group):
    half = len(own) * QB // 2
    span = 2 * half + QB
    lanes = group * QB
    tiles = half // QB
    assert blocks[0].shape[0] == QB
    whole = pl.BlockSpec((half, 2 * HD), lambda t, s: (0, 0))
    pick = [pl.BlockSpec(x.shape, lambda t, s, n=x.ndim: (0,) * n) for x in (*own, *far)]
    buf = [pltpu.VMEM((span, lanes), bf16)] * 4 + [pltpu.VMEM((lanes, 2 * HD), bf16)] * 2
    dq_shape = ((1 + part) * half, group * HD)
    return pl.pallas_call(
        functools.partial(attn_kernel, group, part, len(blocks), len(given)),
        grid_spec=pltpu.PrefetchScalarGridSpec(
            num_scalar_prefetch=1,
            grid=(tiles // 2,),
            in_specs=[
                *[pl.BlockSpec(x.shape, lambda t, s: (0, 0)) for x in blocks],
                *pick, *[pl.BlockSpec(x.shape, lambda t, s: (0, 0)) for x in given],
            ],
            out_specs=[pl.BlockSpec(dq_shape, lambda t, s: (0, 0)), whole, whole, whole],
            scratch_shapes=[
                pltpu.VMEM((3 * half, 2 * HD), bf16),
                pltpu.VMEM((3 * half, 2 * HD), bf16),
                pltpu.VMEM((2 * HD, 3 * half), bf16),
                pltpu.VMEM((3 * half, 2 * HD), f32),
                pltpu.VMEM((3 * half, 2 * HD), f32),
                pltpu.VMEM((span, lanes), f32),
                pltpu.VMEM((span, lanes), f32),
                *buf,
                *buf,
                pltpu.VMEM((tiles, *blocks[0].shape), f32),
            ],
        ),
        out_shape=[
            jax.ShapeDtypeStruct(dq_shape, f32),
            *[jax.ShapeDtypeStruct((half, 2 * HD), f32)] * 3,
        ],
        compiler_params=pltpu.CompilerParams(
            dimension_semantics=("arbitrary",), vmem_limit_bytes=ATTN_VMEM),
    )(place, *blocks, *own, *far, *given)


def spread_kernel(parts, place_ref, *refs):
    ins, outs, sems = refs[:2], refs[2:-1], refs[-1]
    me = place_ref[1]
    copies = []
    for k in range(parts):
        for n, ref in enumerate(ins):
            width = ref.shape[1] // parts
            start = pl.multiple_of((me ^ k) * width, width)
            copies.append(pltpu.make_async_copy(
                ref.at[:, pl.ds(start, width)],
                outs[k].at[:, pl.ds(n * width, width)],
                sems.at[2 * k + n],
            ))
    for copy in copies:
        copy.start()
    for copy in copies:
        copy.wait()


def spread(place, first, second, parts):
    rows, cols = first.shape
    return pl.pallas_call(
        functools.partial(spread_kernel, parts),
        in_specs=[
            pl.BlockSpec(memory_space=pltpu.SMEM),
            pl.BlockSpec(memory_space=pltpu.MemorySpace.HBM),
            pl.BlockSpec(memory_space=pltpu.MemorySpace.HBM),
        ],
        out_specs=[pl.BlockSpec(memory_space=pltpu.VMEM)] * parts,
        out_shape=[jax.ShapeDtypeStruct((rows, 2 * cols // parts), f32)] * parts,
        scratch_shapes=[pltpu.SemaphoreType.DMA((2 * parts,))],
        compiler_params=pltpu.CompilerParams(vmem_limit_bytes=MOVE_VMEM),
    )(place, first, second)


def combine_kernel(place_ref, own_ref, back_ref, *outs):
    me = place_ref[1]
    count = len(outs)
    for j, out in enumerate(outs):
        rows = out.shape[0]
        r = pl.ds(pl.multiple_of(((me ^ j) & (count - 1)) * rows, rows), rows)
        out[...] = own_ref[r, :] + back_ref[r, :]


def combine(place, own, back, count):
    rows, cols = own.shape
    vmem = pl.BlockSpec(memory_space=pltpu.VMEM)
    return pl.pallas_call(
        combine_kernel,
        in_specs=[pl.BlockSpec(memory_space=pltpu.SMEM), vmem, vmem],
        out_specs=[vmem] * count,
        out_shape=[jax.ShapeDtypeStruct((rows // count, cols), f32)] * count,
        compiler_params=pltpu.CompilerParams(vmem_limit_bytes=MOVE_VMEM),
    )(place, own, back)


def unpack_q_kernel(x_ref, out_ref):
    width = x_ref.shape[2]
    for j in range(x_ref.shape[0]):
        out_ref[:, j * width:(j + 1) * width] = x_ref[j]


def unpack_q(x):
    parts, rows, cols = x.shape
    return pl.pallas_call(
        unpack_q_kernel,
        out_shape=jax.ShapeDtypeStruct((rows, parts * cols), f32),
        compiler_params=pltpu.CompilerParams(vmem_limit_bytes=MOVE_VMEM),
        name="unpack_q",
    )(x)


def gather_kernel(parts, place_ref, *refs):
    sets, outs = (refs[:parts], refs[parts:2 * parts]), refs[2 * parts:]
    me = place_ref[1]
    upper = me >= parts // 2
    for n, blocks in enumerate(sets):
        @pl.when(upper if n else jnp.logical_not(upper))
        def _():
            for k, block in enumerate(blocks):
                start = pl.multiple_of((me ^ k) * HD, HD)
                for m, out in enumerate(outs):
                    out[:, pl.ds(start, HD)] = block[:, m * HD:(m + 1) * HD]


def gather(place, lower, upper):
    parts = len(lower)
    rows, _ = lower[0].shape
    vmem = pl.BlockSpec(memory_space=pltpu.VMEM)
    return pl.pallas_call(
        functools.partial(gather_kernel, parts),
        in_specs=[pl.BlockSpec(memory_space=pltpu.SMEM)] + [vmem] * (2 * parts),
        out_specs=[vmem] * 2,
        out_shape=[jax.ShapeDtypeStruct((rows, parts * HD), f32)] * 2,
        compiler_params=pltpu.CompilerParams(vmem_limit_bytes=MOVE_VMEM),
        name="unpack_kv",
    )(place, *lower, *upper)


PLANE = ("inner", "head")


def swap(x):
    return lax.all_to_all(x, PLANE, split_axis=0, concat_axis=0, tiled=True)


def shifted(x, by):
    devices = lax.axis_size("outer")
    return lax.ppermute(x, "outer", [(i, i + by) for i in range(devices) if 0 <= i + by < devices])


def exchanged(x, k, side=None):
    heads, inner = lax.axis_size("head"), lax.axis_size("inner")
    pairs = []
    for h in range(heads):
        for i in range(inner):
            to = (i * heads + h) ^ k
            if side is None or to // heads == side:
                pairs.append((h * inner + i, (to % heads) * inner + to // heads))
    return lax.ppermute(x, ("head", "inner"), pairs)


def staged(query, key_in, value_in, d_out):
    heads = lax.axis_size("head")
    parts = lax.axis_size("inner") * heads
    rows = query.shape[0]
    group = query.shape[1] // key_in.shape[1]
    assert lax.axis_size("inner") == 2 and heads & (heads - 1) == 0
    assert key_in.shape[1] == parts * HD and rows == QB
    me = lax.axis_index("inner") * heads + lax.axis_index("head")
    place = jnp.stack([lax.axis_index("outer"), me]).astype(jnp.int32)
    order = range(parts - 1, 0, -1)
    kv = list(spread(place, key_in, value_in, parts))
    for k in order:
        kv[k] = exchanged(kv[k], k)
    blocks = list(spread(place, query, d_out, parts))
    for k in order:
        blocks[k] = exchanged(blocks[k], k)
    near = shifted(jnp.stack(kv[:2]), 1)
    rest = shifted(jnp.stack(kv[2:]), 1)
    far, own = (near, rest), kv
    dq0, f0, f1, o0 = attn(place, blocks, 0, far, own, (), group)
    back0 = shifted(f0, -1)
    dq, f1, o0, o1 = attn(place, blocks, 1, far, own, (f1, o0, dq0), group)
    back1 = shifted(f1, -1)
    back_q = swap(dq.reshape(parts, rows, group * HD))
    sides = []
    for side, (mine, back) in enumerate(((o0, back0), (o1, back1))):
        sums = combine(place, mine, back, heads)
        got = [sums[0]]
        for k in range(1, parts):
            got.append(exchanged(sums[k % heads], k, side))
        sides.append(got)
    grad_query = unpack_q(back_q)
    grad_key, grad_value = gather(place, *sides)
    return grad_query, grad_key, grad_value


def solution(mesh):
    assert mesh.axis_names == ("head", "seq")
    heads, seqs = mesh.devices.shape

    def run(query, key_in, value_in, d_out):
        shard = query.shape[0] // seqs
        inner = WINDOW // shard
        fine = jax.sharding.Mesh(
            mesh.devices.reshape(heads, seqs // inner, inner), ("head", "outer", "inner")
        )
        spec = P(("outer", "inner", "head"), None)
        step = jax.shard_map(
            staged, mesh=fine, in_specs=(spec,) * 4, out_specs=(spec,) * 3, check_vma=False
        )
        return step(query, key_in, value_in, d_out)

    return run
```

profile of v0, /device:TPU:0, one launch (start us, length us, event | category | flops | bytes accessed | tf_op | source)
XLA Modules:
  0.0 133.3 jit_solution(15357587806365047169)
XLA Ops:
  3.7 3.0 %collective-permute-start.8 = (f32[128,256]{1,0:T(8,128)S(1)}, f32[128,256]{1,0:T(8,128)S(1)}, u32[]{:S(2)}, u32[]{:S(2)}) collective-permute-start(f32[128,256]{1,0:T(8,128)S(1)} %get-tuple-element.47), channel_id=1, source_target_pairs={{0,16},{1,17},{8,24},{9,25},{16,0},{17,1},{24,8},{25,9},{2,18},{3,... | collective-permute-start | bytes 393224 | tf_op jit(solution)/shard_map/ppermute | solution.py:375
  8.5 2.7 %collective-permute-start.12 = (f32[128,256]{1,0:T(8,128)S(1)}, f32[128,256]{1,0:T(8,128)S(1)}, u32[]{:S(2)}, u32[]{:S(2)}) collective-permute-start(f32[128,256]{1,0:T(8,128)S(1)} %get-tuple-element.51), channel_id=1, source_target_pairs={{0,17},{1,16},{8,25},{9,24},{16,1},{17,0},{24,9},{25,8},{2,19},{3,... | collective-permute-start | bytes 393224 | tf_op jit(solution)/shard_map/ppermute | solution.py:375
  11.5 1.9 %collective-permute-done.9.refs_11_ = f32[128,256]{1,0:T(8,128)S(1)} collective-permute-done((f32[128,256]{1,0:T(8,128)S(1)}, f32[128,256]{1,0:T(8,128)S(1)}, u32[]{:S(2)}, u32[]{:S(2)}) %collective-permute-start.9) | collective-permute-done | bytes 131104 | tf_op jit(solution)/shard_map/ppermute | solution.py:375
  13.5 7.0 %collective-permute-done.11.refs_13_ = f32[128,256]{1,0:T(8,128)S(1)} collective-permute-done((f32[128,256]{1,0:T(8,128)S(1)}, f32[128,256]{1,0:T(8,128)S(1)}, u32[]{:S(2)}, u32[]{:S(2)}) %collective-permute-start.11) | collective-permute-done | bytes 131104 | tf_op jit(solution)/shard_map/ppermute | solution.py:375
  20.5 4.0 %collective-permute-start.15 = (f32[6,128,256]{2,1,0:T(8,128)S(1)}, f32[6,128,256]{2,1,0:T(8,128)S(1)}, u32[]{:S(2)}, u32[]{:S(2)}) collective-permute-start(f32[6,128,256]{2,1,0:T(8,128)S(1)} %bitcast_dynamic-update-slice_fusion), channel_id=1, source_target_pairs={{0,2},{2,4},{4,6},{1,3},{3,5},{5,7},{8,10},{10,12},{12,14},{9,11},... | collective-permute-start | bytes 2359304 | tf_op jit(solution)/shard_map/ppermute | solution.py:364
  26.2 1.8 %collective-permute-start.1 = (f32[128,512]{1,0:T(8,128)S(1)}, f32[128,512]{1,0:T(8,128)S(1)}, u32[]{:S(2)}, u32[]{:S(2)}) collective-permute-start(f32[128,512]{1,0:T(8,128)S(1)} %get-tuple-element.39), channel_id=1, source_target_pairs={{0,16},{1,17},{8,24},{9,25},{16,0},{17,1},{24,8},{25,9},{2,18},{3,... | collective-permute-start | bytes 786440 | tf_op jit(solution)/shard_map/ppermute | solution.py:375
  29.8 5.6 %collective-permute-done.1.refs_2_ = f32[128,512]{1,0:T(8,128)S(1)} collective-permute-done((f32[128,512]{1,0:T(8,128)S(1)}, f32[128,512]{1,0:T(8,128)S(1)}, u32[]{:S(2)}, u32[]{:S(2)}) %collective-permute-start.1) | collective-permute-done | bytes 262176 | tf_op jit(solution)/shard_map/ppermute | solution.py:375
  35.4 2.8 %collective-permute-start.5 = (f32[128,512]{1,0:T(8,128)S(1)}, f32[128,512]{1,0:T(8,128)S(1)}, u32[]{:S(2)}, u32[]{:S(2)}) collective-permute-start(f32[128,512]{1,0:T(8,128)S(1)} %get-tuple-element.43), channel_id=1, source_target_pairs={{0,17},{1,16},{8,25},{9,24},{16,1},{17,0},{24,9},{25,8},{2,19},{3,... | collective-permute-start | bytes 786440 | tf_op jit(solution)/shard_map/ppermute | solution.py:375
  38.1 2.2 %collective-permute-done.2.refs_3_ = f32[128,512]{1,0:T(8,128)S(1)} collective-permute-done((f32[128,512]{1,0:T(8,128)S(1)}, f32[128,512]{1,0:T(8,128)S(1)}, u32[]{:S(2)}, u32[]{:S(2)}) %collective-permute-start.2) | collective-permute-done | bytes 262176 | tf_op jit(solution)/shard_map/ppermute | solution.py:375
  40.3 3.2 %collective-permute-start.6 = (f32[128,512]{1,0:T(8,128)S(1)}, f32[128,512]{1,0:T(8,128)S(1)}, u32[]{:S(2)}, u32[]{:S(2)}) collective-permute-start(f32[128,512]{1,0:T(8,128)S(1)} %get-tuple-element.44), channel_id=1, source_target_pairs={{0,25},{1,24},{8,17},{9,16},{16,9},{17,8},{24,1},{25,0},{2,27},{3,... | collective-permute-start | bytes 786440 | tf_op jit(solution)/shard_map/ppermute | solution.py:375
  43.5 3.4 %collective-permute-start.14 = (f32[2,128,256]{2,1,0:T(8,128)S(1)}, f32[2,128,256]{2,1,0:T(8,128)S(1)}, u32[]{:S(2)}, u32[]{:S(2)}) collective-permute-start(f32[2,128,256]{2,1,0:T(8,128)S(1)} %pad_maximum_fusion), channel_id=1, source_target_pairs={{0,2},{2,4},{4,6},{1,3},{3,5},{5,7},{8,10},{10,12},{12,14},{9,11},... | collective-permute-start | bytes 786440 | tf_op jit(solution)/shard_map/ppermute | solution.py:364
  46.9 5.9 %collective-permute-done.4.refs_5_ = f32[128,512]{1,0:T(8,128)S(1)} collective-permute-done((f32[128,512]{1,0:T(8,128)S(1)}, f32[128,512]{1,0:T(8,128)S(1)}, u32[]{:S(2)}, u32[]{:S(2)}) %collective-permute-start.4) | collective-permute-done | bytes 262176 | tf_op jit(solution)/shard_map/ppermute | solution.py:375
  52.8 11.1 %shard_map.69 = (f32[512,256]{1,0:T(8,128)S(1)}, f32[512,256]{1,0:T(8,128)S(1)}, f32[512,256]{1,0:T(8,128)S(1)}, f32[512,256]{1,0:T(8,128)S(1)}) custom-call(s32[2]{0:T(128)S(1)} %pad_add_fusion.place_ref, f32[128,512]{1,0:T(8,128)S(1)} %get-tuple-element.37.refs_0_, f32[128,512]{1,0:T(8,128)S(1)} %collective-permute-done.refs_1_, ...), custom_call_target="tpu_custom_call" | custom-call | tf_op jit(solution)/shard_map/pallas_call | solution.py:224
  63.9 12.3 %shard_map.70 = (f32[1024,256]{1,0:T(8,128)}, f32[512,256]{1,0:T(8,128)}, f32[512,256]{1,0:T(8,128)S(1)}, f32[512,256]{1,0:T(8,128)S(1)}) custom-call(s32[2]{0:T(128)S(1)} %pad_add_fusion.place_ref, f32[128,512]{1,0:T(8,128)S(1)} %get-tuple-element.37.refs_0_, f32[128,512]{1,0:T(8,128)S(1)} %collective-permute-done.refs_1_, ...), custom_call_target="tpu_custom_call" | custom-call | tf_op jit(solution)/shard_map/pallas_call | solution.py:224
  77.5 4.4 %all-to-all-start = ((f32[8,128,256]{2,1,0:T(8,128)}), f32[8,128,256]{2,1,0:T(8,128)S(1)}, u32[]{:S(2)}, u32[]{:S(2)}) async-start(f32[8,128,256]{2,1,0:T(8,128)} %bitcast.10), calls=%async_computation | async-start | bytes 2097152 | tf_op jit(solution)/shard_map/all_to_all | solution.py:359
  83.2 9.9 %collective-permute-done.24.back_ref = f32[512,256]{1,0:T(8,128)S(1)} collective-permute-done((f32[512,256]{1,0:T(8,128)}, f32[512,256]{1,0:T(8,128)S(1)}, u32[]{:S(2)}, u32[]{:S(2)}) %collective-permute-start.24) | collective-permute-done | bytes 524320 | tf_op jit(solution)/shard_map/ppermute | solution.py:364
  93.7 3.4 %collective-permute-start.28 = (f32[128,256]{1,0:T(8,128)S(1)}, f32[128,256]{1,0:T(8,128)S(1)}, u32[]{:S(2)}, u32[]{:S(2)}) collective-permute-start(f32[128,256]{1,0:T(8,128)S(1)} %get-tuple-element.65.refs_8_), channel_id=1, source_target_pairs={{0,1},{8,9},{16,17},{24,25},{2,3},{10,11},{18,19},{26,27},{4,5},{1... | collective-permute-start | bytes 393224 | tf_op jit(solution)/shard_map/ppermute | solution.py:375
  99.2 4.1 %collective-permute-start.30 = (f32[128,256]{1,0:T(8,128)S(1)}, f32[128,256]{1,0:T(8,128)S(1)}, u32[]{:S(2)}, u32[]{:S(2)}) collective-permute-start(f32[128,256]{1,0:T(8,128)S(1)} %get-tuple-element.67), channel_id=1, source_target_pairs={{0,17},{8,25},{16,1},{24,9},{2,19},{10,27},{18,3},{26,11},{4,21},{... | collective-permute-start | bytes 393224 | tf_op jit(solution)/shard_map/ppermute | solution.py:375
  105.2 5.1 %collective-permute-start.31 = (f32[128,256]{1,0:T(8,128)S(1)}, f32[128,256]{1,0:T(8,128)S(1)}, u32[]{:S(2)}, u32[]{:S(2)}) collective-permute-start(f32[128,256]{1,0:T(8,128)S(1)} %get-tuple-element.68), channel_id=1, source_target_pairs={{0,25},{8,17},{16,9},{24,1},{2,27},{10,19},{18,11},{26,3},{4,29},{... | collective-permute-start | bytes 393224 | tf_op jit(solution)/shard_map/ppermute | solution.py:375
  113.5 3.1 %collective-permute-start.17 = (f32[128,256]{1,0:T(8,128)S(1)}, f32[128,256]{1,0:T(8,128)S(1)}, u32[]{:S(2)}, u32[]{:S(2)}) collective-permute-start(f32[128,256]{1,0:T(8,128)S(1)} %get-tuple-element.60), channel_id=1, source_target_pairs={{0,8},{8,0},{16,24},{24,16},{2,10},{10,2},{18,26},{26,18},{4,12},{... | collective-permute-start | bytes 393224 | tf_op jit(solution)/shard_map/ppermute | solution.py:375
  118.0 3.7 %collective-permute-start.18 = (f32[128,256]{1,0:T(8,128)S(1)}, f32[128,256]{1,0:T(8,128)S(1)}, u32[]{:S(2)}, u32[]{:S(2)}) collective-permute-start(f32[128,256]{1,0:T(8,128)S(1)} %get-tuple-element.61), channel_id=1, source_target_pairs={{0,16},{8,24},{16,0},{24,8},{2,18},{10,26},{18,2},{26,10},{4,20},{... | collective-permute-start | bytes 393224 | tf_op jit(solution)/shard_map/ppermute | solution.py:375
  123.0 1.9 %collective-permute-start.19 = (f32[128,256]{1,0:T(8,128)S(1)}, f32[128,256]{1,0:T(8,128)S(1)}, u32[]{:S(2)}, u32[]{:S(2)}) collective-permute-start(f32[128,256]{1,0:T(8,128)S(1)} %get-tuple-element.62), channel_id=1, source_target_pairs={{0,24},{8,16},{16,8},{24,0},{2,26},{10,18},{18,10},{26,2},{4,28},{... | collective-permute-start | bytes 393224 | tf_op jit(solution)/shard_map/ppermute | solution.py:375
  125.4 4.9 %collective-permute-done.23.refs_7_ = f32[128,256]{1,0:T(8,128)S(1)} collective-permute-done((f32[128,256]{1,0:T(8,128)S(1)}, f32[128,256]{1,0:T(8,128)S(1)}, u32[]{:S(2)}, u32[]{:S(2)}) %collective-permute-start.23) | collective-permute-done | bytes 131104 | tf_op jit(solution)/shard_map/ppermute | solution.py:375
  130.6 1.6 %unpack_kv.1 = (f32[128,1024]{1,0:T(8,128)}, f32[128,1024]{1,0:T(8,128)}) custom-call(s32[2]{0:T(128)S(1)} %pad_add_fusion.place_ref, f32[128,256]{1,0:T(8,128)S(1)} %get-tuple-element.59.refs_0_, f32[128,256]{1,0:T(8,128)S(1)} %collective-permute-done.17.refs_1_, f32[128,256]{1,0:T(8,128)S(1)} %collective-permute-done.18.refs_2_, ...), custom_call_target="tpu_custom_call" | custom-call | tf_op jit(solution)/shard_map/unpack_kv/pallas_call | solution.py:345
  (66 shorter events, 23.4 us)
Async XLA Ops:
  8.3 12.2 %collective-permute-start.11 = (f32[128,256]{1,0:T(8,128)S(1)}, f32[128,256]{1,0:T(8,128)S(1)}, u32[]{:S(2)}, u32[]{:S(2)}) collective-permute-start(f32[128,256]{1,0:T(8,128)S(1)} %get-tuple-element.50), channel_id=1, source_target_pairs={{0,9},{1,8},{8,1},{9,0},{16,25},{17,24},{24,17},{25,16},{2,11},{3,... | collective-permute-start | bytes 393224 | tf_op jit(solution)/shard_map/ppermute | solution.py:375
  8.5 11.9 %collective-permute-start.12 = (f32[128,256]{1,0:T(8,128)S(1)}, f32[128,256]{1,0:T(8,128)S(1)}, u32[]{:S(2)}, u32[]{:S(2)}) collective-permute-start(f32[128,256]{1,0:T(8,128)S(1)} %get-tuple-element.51), channel_id=1, source_target_pairs={{0,17},{1,16},{8,25},{9,24},{16,1},{17,0},{24,9},{25,8},{2,19},{3,... | collective-permute-start | bytes 393224 | tf_op jit(solution)/shard_map/ppermute | solution.py:375
  11.2 9.3 %collective-permute-start.13 = (f32[128,256]{1,0:T(8,128)S(1)}, f32[128,256]{1,0:T(8,128)S(1)}, u32[]{:S(2)}, u32[]{:S(2)}) collective-permute-start(f32[128,256]{1,0:T(8,128)S(1)} %get-tuple-element.52), channel_id=1, source_target_pairs={{0,25},{1,24},{8,17},{9,16},{16,9},{17,8},{24,1},{25,0},{2,27},{3,... | collective-permute-start | bytes 393224 | tf_op jit(solution)/shard_map/ppermute | solution.py:375
  20.5 32.3 %collective-permute-start.15 = (f32[6,128,256]{2,1,0:T(8,128)S(1)}, f32[6,128,256]{2,1,0:T(8,128)S(1)}, u32[]{:S(2)}, u32[]{:S(2)}) collective-permute-start(f32[6,128,256]{2,1,0:T(8,128)S(1)} %bitcast_dynamic-update-slice_fusion), channel_id=1, source_target_pairs={{0,2},{2,4},{4,6},{1,3},{3,5},{5,7},{8,10},{10,12},{12,14},{9,11},... | collective-permute-start | bytes 2359304 | tf_op jit(solution)/shard_map/ppermute | solution.py:364
  26.2 9.2 %collective-permute-start.1 = (f32[128,512]{1,0:T(8,128)S(1)}, f32[128,512]{1,0:T(8,128)S(1)}, u32[]{:S(2)}, u32[]{:S(2)}) collective-permute-start(f32[128,512]{1,0:T(8,128)S(1)} %get-tuple-element.39), channel_id=1, source_target_pairs={{0,16},{1,17},{8,24},{9,25},{16,0},{17,1},{24,8},{25,9},{2,18},{3,... | collective-permute-start | bytes 786440 | tf_op jit(solution)/shard_map/ppermute | solution.py:375
  28.0 12.3 %collective-permute-start.2 = (f32[128,512]{1,0:T(8,128)S(1)}, f32[128,512]{1,0:T(8,128)S(1)}, u32[]{:S(2)}, u32[]{:S(2)}) collective-permute-start(f32[128,512]{1,0:T(8,128)S(1)} %get-tuple-element.40), channel_id=1, source_target_pairs={{0,24},{1,25},{8,16},{9,17},{16,8},{17,9},{24,0},{25,1},{2,26},{3,... | collective-permute-start | bytes 786440 | tf_op jit(solution)/shard_map/ppermute | solution.py:375
  28.0 15.5 %collective-permute-start.3 = (f32[128,512]{1,0:T(8,128)S(1)}, f32[128,512]{1,0:T(8,128)S(1)}, u32[]{:S(2)}, u32[]{:S(2)}) collective-permute-start(f32[128,512]{1,0:T(8,128)S(1)} %get-tuple-element.41), channel_id=1, source_target_pairs={{0,1},{1,0},{8,9},{9,8},{16,17},{17,16},{24,25},{25,24},{2,3},{3,2... | collective-permute-start | bytes 786440 | tf_op jit(solution)/shard_map/ppermute | solution.py:375
  29.6 23.2 %collective-permute-start.4 = (f32[128,512]{1,0:T(8,128)S(1)}, f32[128,512]{1,0:T(8,128)S(1)}, u32[]{:S(2)}, u32[]{:S(2)}) collective-permute-start(f32[128,512]{1,0:T(8,128)S(1)} %get-tuple-element.42), channel_id=1, source_target_pairs={{0,9},{1,8},{8,1},{9,0},{16,25},{17,24},{24,17},{25,16},{2,11},{3,... | collective-permute-start | bytes 786440 | tf_op jit(solution)/shard_map/ppermute | solution.py:375
  35.4 17.4 %collective-permute-start.5 = (f32[128,512]{1,0:T(8,128)S(1)}, f32[128,512]{1,0:T(8,128)S(1)}, u32[]{:S(2)}, u32[]{:S(2)}) collective-permute-start(f32[128,512]{1,0:T(8,128)S(1)} %get-tuple-element.43), channel_id=1, source_target_pairs={{0,17},{1,16},{8,25},{9,24},{16,1},{17,0},{24,9},{25,8},{2,19},{3,... | collective-permute-start | bytes 786440 | tf_op jit(solution)/shard_map/ppermute | solution.py:375
  40.3 12.5 %collective-permute-start.6 = (f32[128,512]{1,0:T(8,128)S(1)}, f32[128,512]{1,0:T(8,128)S(1)}, u32[]{:S(2)}, u32[]{:S(2)}) collective-permute-start(f32[128,512]{1,0:T(8,128)S(1)} %get-tuple-element.44), channel_id=1, source_target_pairs={{0,25},{1,24},{8,17},{9,16},{16,9},{17,8},{24,1},{25,0},{2,27},{3,... | collective-permute-start | bytes 786440 | tf_op jit(solution)/shard_map/ppermute | solution.py:375
  43.5 9.3 %collective-permute-start.14 = (f32[2,128,256]{2,1,0:T(8,128)S(1)}, f32[2,128,256]{2,1,0:T(8,128)S(1)}, u32[]{:S(2)}, u32[]{:S(2)}) collective-permute-start(f32[2,128,256]{2,1,0:T(8,128)S(1)} %pad_maximum_fusion), channel_id=1, source_target_pairs={{0,2},{2,4},{4,6},{1,3},{3,5},{5,7},{8,10},{10,12},{12,14},{9,11},... | collective-permute-start | bytes 786440 | tf_op jit(solution)/shard_map/ppermute | solution.py:364
  76.3 16.9 %collective-permute-start.24 = (f32[512,256]{1,0:T(8,128)}, f32[512,256]{1,0:T(8,128)S(1)}, u32[]{:S(2)}, u32[]{:S(2)}) collective-permute-start(f32[512,256]{1,0:T(8,128)} %get-tuple-element.64), channel_id=1, source_target_pairs={{2,0},{4,2},{6,4},{3,1},{5,3},{7,5},{10,8},{12,10},{14,12},{11,9},... | collective-permute-start | bytes 1572872 | tf_op jit(solution)/shard_map/ppermute | solution.py:364
  77.5 54.7 %all-to-all-start = ((f32[8,128,256]{2,1,0:T(8,128)}), f32[8,128,256]{2,1,0:T(8,128)S(1)}, u32[]{:S(2)}, u32[]{:S(2)}) async-start(f32[8,128,256]{2,1,0:T(8,128)} %bitcast.10), calls=%async_computation | async-start | bytes 2097152 | tf_op jit(solution)/shard_map/all_to_all | solution.py:359
  81.9 21.9 %collective-permute-start.16 = (f32[512,256]{1,0:T(8,128)S(1)}, f32[512,256]{1,0:T(8,128)S(1)}, u32[]{:S(2)}, u32[]{:S(2)}) collective-permute-start(f32[512,256]{1,0:T(8,128)S(1)} %get-tuple-element.58), channel_id=1, source_target_pairs={{2,0},{4,2},{6,4},{3,1},{5,3},{7,5},{10,8},{12,10},{14,12},{11,9},... | collective-permute-start | bytes 1572872 | tf_op jit(solution)/shard_map/ppermute | solution.py:364
  93.7 11.4 %collective-permute-start.28 = (f32[128,256]{1,0:T(8,128)S(1)}, f32[128,256]{1,0:T(8,128)S(1)}, u32[]{:S(2)}, u32[]{:S(2)}) collective-permute-start(f32[128,256]{1,0:T(8,128)S(1)} %get-tuple-element.65.refs_8_), channel_id=1, source_target_pairs={{0,1},{8,9},{16,17},{24,25},{2,3},{10,11},{18,19},{26,27},{4,5},{1... | collective-permute-start | bytes 393224 | tf_op jit(solution)/shard_map/ppermute | solution.py:375
  97.2 13.0 %collective-permute-start.29 = (f32[128,256]{1,0:T(8,128)S(1)}, f32[128,256]{1,0:T(8,128)S(1)}, u32[]{:S(2)}, u32[]{:S(2)}) collective-permute-start(f32[128,256]{1,0:T(8,128)S(1)} %get-tuple-element.66), channel_id=1, source_target_pairs={{0,9},{8,1},{16,25},{24,17},{2,11},{10,3},{18,27},{26,19},{4,13},{... | collective-permute-start | bytes 393224 | tf_op jit(solution)/shard_map/ppermute | solution.py:375
  98.5 12.4 %collective-permute-start.25 = (f32[128,256]{1,0:T(8,128)S(1)}, f32[128,256]{1,0:T(8,128)S(1)}, u32[]{:S(2)}, u32[]{:S(2)}) collective-permute-start(f32[128,256]{1,0:T(8,128)S(1)} %get-tuple-element.66), channel_id=1, source_target_pairs={{1,9},{9,1},{17,25},{25,17},{3,11},{11,3},{19,27},{27,19},{5,13},{... | collective-permute-start | bytes 393224 | tf_op jit(solution)/shard_map/ppermute | solution.py:375
  99.2 13.1 %collective-permute-start.30 = (f32[128,256]{1,0:T(8,128)S(1)}, f32[128,256]{1,0:T(8,128)S(1)}, u32[]{:S(2)}, u32[]{:S(2)}) collective-permute-start(f32[128,256]{1,0:T(8,128)S(1)} %get-tuple-element.67), channel_id=1, source_target_pairs={{0,17},{8,25},{16,1},{24,9},{2,19},{10,27},{18,3},{26,11},{4,21},{... | collective-permute-start | bytes 393224 | tf_op jit(solution)/shard_map/ppermute | solution.py:375
  103.9 9.7 %collective-permute-start.26 = (f32[128,256]{1,0:T(8,128)S(1)}, f32[128,256]{1,0:T(8,128)S(1)}, u32[]{:S(2)}, u32[]{:S(2)}) collective-permute-start(f32[128,256]{1,0:T(8,128)S(1)} %get-tuple-element.67), channel_id=1, source_target_pairs={{1,17},{9,25},{17,1},{25,9},{3,19},{11,27},{19,3},{27,11},{5,21},{... | collective-permute-start | bytes 393224 | tf_op jit(solution)/shard_map/ppermute | solution.py:375
  105.2 11.5 %collective-permute-start.31 = (f32[128,256]{1,0:T(8,128)S(1)}, f32[128,256]{1,0:T(8,128)S(1)}, u32[]{:S(2)}, u32[]{:S(2)}) collective-permute-start(f32[128,256]{1,0:T(8,128)S(1)} %get-tuple-element.68), channel_id=1, source_target_pairs={{0,25},{8,17},{16,9},{24,1},{2,27},{10,19},{18,11},{26,3},{4,29},{... | collective-permute-start | bytes 393224 | tf_op jit(solution)/shard_map/ppermute | solution.py:375
  110.9 10.8 %collective-permute-start.20 = (f32[128,256]{1,0:T(8,128)S(1)}, f32[128,256]{1,0:T(8,128)S(1)}, u32[]{:S(2)}, u32[]{:S(2)}) collective-permute-start(f32[128,256]{1,0:T(8,128)S(1)} %get-tuple-element.59.refs_0_), channel_id=1, source_target_pairs={{1,0},{9,8},{17,16},{25,24},{3,2},{11,10},{19,18},{27,26},{5,4},{1... | collective-permute-start | bytes 393224 | tf_op jit(solution)/shard_map/ppermute | solution.py:375
  112.2 10.8 %collective-permute-start.21 = (f32[128,256]{1,0:T(8,128)S(1)}, f32[128,256]{1,0:T(8,128)S(1)}, u32[]{:S(2)}, u32[]{:S(2)}) collective-permute-start(f32[128,256]{1,0:T(8,128)S(1)} %get-tuple-element.60), channel_id=1, source_target_pairs={{1,8},{9,0},{17,24},{25,16},{3,10},{11,2},{19,26},{27,18},{5,12},{... | collective-permute-start | bytes 393224 | tf_op jit(solution)/shard_map/ppermute | solution.py:375
  113.5 11.4 %collective-permute-start.17 = (f32[128,256]{1,0:T(8,128)S(1)}, f32[128,256]{1,0:T(8,128)S(1)}, u32[]{:S(2)}, u32[]{:S(2)}) collective-permute-start(f32[128,256]{1,0:T(8,128)S(1)} %get-tuple-element.60), channel_id=1, source_target_pairs={{0,8},{8,0},{16,24},{24,16},{2,10},{10,2},{18,26},{26,18},{4,12},{... | collective-permute-start | bytes 393224 | tf_op jit(solution)/shard_map/ppermute | solution.py:375
  121.7 8.5 %collective-permute-start.23 = (f32[128,256]{1,0:T(8,128)S(1)}, f32[128,256]{1,0:T(8,128)S(1)}, u32[]{:S(2)}, u32[]{:S(2)}) collective-permute-start(f32[128,256]{1,0:T(8,128)S(1)} %get-tuple-element.62), channel_id=1, source_target_pairs={{1,24},{9,16},{17,8},{25,0},{3,26},{11,18},{19,10},{27,2},{5,28},{... | collective-permute-start | bytes 393224 | tf_op jit(solution)/shard_map/ppermute | solution.py:375
  (13 other events, 104.1 us)
where the time goes:
time: 134 us; the launch traced here: 133 us
  starting transfers between devices  62.1 us (46%)
  waiting for transfers between devices  38.7 us (29%)
  Pallas kernels  29.3 us (22%)
  local copies, waits for them, and re-layouts  2.16 us (2%)
    ppermute x28, starting transfers between devices, exchanged(): return lax.ppermute(x, ('head', 'inner'), pairs)  47.7 us
    ppermute x28, waiting for transfers between devices, exchanged(): return lax.ppermute(x, ('head', 'inner'), pairs)  28.2 us
    pallas_call x2, Pallas kernels, attn(): pl.pallas_call(functools.partial(attn_kernel, group, part, len(blocks), l...  23.4 us
    ppermute x4, waiting for transfers between devices, shifted(): lax.ppermute(x, 'outer', [(i, i + by) for i in range(devices) if 0 <= i +...  10.5 us
    ppermute x4, starting transfers between devices, shifted(): lax.ppermute(x, 'outer', [(i, i + by) for i in range(devices) if 0 <= i +...  9.98 us
    all_to_all x1, starting transfers between devices, swap(): return lax.all_to_all(x, PLANE, split_axis=0, concat_axis=0, tiled=True)  4.4 us
  transfers between devices with their start and end apart: 33, of which 10 were waited for; matrix products, arithmetic and copies ran while one was open for 0% of the time, Pallas kernels for 3%

commit v1 on v0

--- a/solution.py
+++ b/solution.py
@@ -39,97 +39,74 @@
 
 QB = 128
 KC = 64
-
-
-def attn_kernel(
-    group, stage, parts, carried, place_ref, *refs,
-):
+MC = 192
+PC = 256
+
+
+def attn_kernel(group, stage, parts, carried, place_ref, *refs):
     blocks, refs = refs[:parts], refs[parts:]
     own, refs = refs[:parts], refs[parts:]
     near, rest, refs = refs[0], refs[1], refs[2:]
     given, refs = refs[:carried], refs[carried:]
     dq_ref, refs = refs[0], refs[1:]
     grads, refs = refs[:3], refs[3:]
-    kaug, vaug, kt, dkacc, dvacc, sref, dpref = refs[:7]
-    bufs, qbuf = refs[7:-1], refs[-1]
+    kaug, vaug, kt, dkacc, dvacc, qbuf, qall, oall = refs[:8]
+    refs = refs[8:]
+    size = len(refs) // 2
+    sets = (refs[:size], refs[size:])
     me = place_ref[1]
-    u = pl.program_id(0)
-    steps = pl.num_programs(0)
+    first = place_ref[0] == 0
     tokens = parts * QB
     half = tokens // 2
+    count = parts // 2
     done_rows = stage * half
     span = tokens + QB
-    far_tiles = parts - stage * (parts // 2)
+    far_tiles = parts - stage * count
     lanes = group * QB
-    sets = (bufs[:6], bufs[6:])
-    first = place_ref[0] == 0
-
-    @pl.when(u == 0)
-    def _():
-        count = parts // 2
-        same = (me < count) == (stage == 0)
-
-        def far_block(k):
-            return near[k] if k < near.shape[0] else rest[k - near.shape[0]]
-
-        def own_block(k):
-            return own[k][...]
-
-        def place_keys(kv, r):
-            r = pl.multiple_of(r, QB)
-            k = kv[:, :HD]
-            hi, lo = split(k)
-            kaug[pl.ds(r, QB), :HD] = hi
-            kaug[pl.ds(r, QB), HD:] = lo
-            vh, vl = split(kv[:, HD:])
-            vaug[pl.ds(r, QB), :HD] = vh
-            vaug[pl.ds(r, QB), HD:] = vl
-            th, tl = split(k.T)
-            kt[:HD, pl.ds(r, QB)] = th
-            kt[HD:, pl.ds(r, QB)] = tl
-
-        full, part = (far_block, own_block) if stage == 0 else (own_block, far_block)
-        full_base, part_base = (0, tokens) if stage == 0 else (half, 0)
-        for k in range(parts):
-            place_keys(full(k), full_base + (me ^ k) * QB)
-        for j in range(count):
-            slot = (me ^ j) & (count - 1)
-            place_keys(jnp.where(same, part(j), part(count + j)), part_base + slot * QB)
-            qbuf[slot] = jnp.where(same, blocks[j][...], blocks[count + j][...])
-        dkacc[...] = jnp.zeros_like(dkacc)
-        dvacc[...] = jnp.zeros_like(dvacc)
-        for buf in sets[1]:
-            buf[...] = jnp.zeros_like(buf)
-        if done_rows:
-            dq_ref[:done_rows, :] = given[-1][...]
+    same = (me < count) == (stage == 0)
+
+    def far_block(k):
+        return near[k] if k < near.shape[0] else rest[k - near.shape[0]]
+
+    def own_block(k):
+        return own[k][...]
+
+    def place_keys(kv, r):
+        r = pl.multiple_of(r, QB)
+        k = kv[:, :HD]
+        hi, lo = split(k)
+        kaug[pl.ds(r, QB), :HD] = hi
+        kaug[pl.ds(r, QB), HD:] = lo
+        vh, vl = split(kv[:, HD:])
+        vaug[pl.ds(r, QB), :HD] = vh
+        vaug[pl.ds(r, QB), HD:] = vl
+        th, tl = split(k.T)
+        kt[:HD, pl.ds(r, QB)] = th
+        kt[HD:, pl.ds(r, QB)] = tl
+
+    full, part = (far_block, own_block) if stage == 0 else (own_block, far_block)
+    full_base, part_base = (0, tokens) if stage == 0 else (half, 0)
+    for k in range(parts):
+        place_keys(full(k), full_base + (me ^ k) * QB)
+    for j in range(count):
+        slot = (me ^ j) & (count - 1)
+        place_keys(jnp.where(same, part(j), part(count + j)), part_base + slot * QB)
+        qbuf[slot] = jnp.where(same, blocks[j][...], blocks[count + j][...])
+    if done_rows:
+        dq_ref[:done_rows, :] = given[-1][...]
 
     rows = lax.broadcasted_iota(jnp.int32, (KC, lanes), 0)
     cols = lax.rem(lax.broadcasted_iota(jnp.int32, (KC, lanes), 1), QB)
 
-    def products(tile, buf):
-        phi, plo, dshi, dslo, qq, oo = buf
-        a = pl.multiple_of(jnp.maximum(tile, 0) * QB, QB)
-        q2 = qq[...]
-        o2 = oo[...]
-        for c in range(0, span, 192):
-            dvacc[pl.ds(a + c, 192), :] += dot(phi[c:c + 192, :], o2) + dot(plo[c:c + 192, :], o2)
-        for c in range(0, span, 192):
-            dkacc[pl.ds(a + c, 192), :] += dot(dshi[c:c + 192, :], q2) + dot(dslo[c:c + 192, :], q2)
-        kts = kt[:, pl.ds(a, span)]
-        full = dot(kts, dshi[...]) + dot(kts, dslo[...])
-        dqt = (full[:HD] + full[HD:]) * score_scale
-        for h in range(group):
-            dq_ref[pl.ds(done_rows + a, QB), h * HD:(h + 1) * HD] = dqt[:, h * QB:(h + 1) * QB].T
-
-    def weights(tile, buf):
-        slot = tile
-        phi, plo, dshi, dslo, qq, oo = buf
-        a = pl.multiple_of(tile * QB, QB)
+    def scores(tile):
+        sref, dpref = sets[tile % 2][:2]
+        qq, oo = qall.at[tile], oall.at[tile]
+        a = tile * QB
         qts = []
         ots = []
         for h in range(group):
-            q = qbuf[slot, :, h * HD:(h + 1) * HD] * (score_scale * LOG2E)
-            o = qbuf[slot, :, (group + h) * HD:(group + h + 1) * HD]
+            q = qbuf[tile, :, h * HD:(h + 1) * HD] * (score_scale * LOG2E)
+            o = qbuf[tile, :, (group + h) * HD:(group + h + 1) * HD]
             qh, ql = split(q)
             oh, ol = split(o)
             qq[h * QB:(h + 1) * QB, :HD] = qh
@@ -144,12 +121,15 @@
         qll = jnp.concatenate([qtl, qtl], axis=0)
         ohh = jnp.concatenate([oth, oth], axis=0)
         oll = jnp.concatenate([otl, otl], axis=0)
-        for c in range(0, span, 192):
-            ka = kaug[pl.ds(a + c, 192), :]
-            sref[c:c + 192, :] = dot(ka, qhh) + dot(ka, qll)
-        for c in range(0, span, 192):
-            va = vaug[pl.ds(a + c, 192), :]
-            dpref[c:c + 192, :] = dot(va, ohh) + dot(va, oll)
+        for c in range(0, span, MC):
+            ka = kaug[a + c:a + c + MC, :]
+            sref[c:c + MC, :] = dot(ka, qhh) + dot(ka, qll)
+        for c in range(0, span, MC):
+            va = vaug[a + c:a + c + MC, :]
+            dpref[c:c + MC, :] = dot(va, ohh) + dot(va, oll)
+
+    def softmax(tile):
+        sref, dpref, phi, plo, dshi, dslo = sets[tile % 2]
 
         def masked(c):
             s = sref[c:c + KC, :]
@@ -159,21 +139,19 @@
                 s = jnp.where(rows + (c - tokens) <= cols, s, -jnp.inf)
             return s
 
-        def is_far(c):
-            return jnp.logical_and(first, tile + c // QB < far_tiles)
-
-        top = jnp.full((8, lanes), -jnp.inf, f32)
-        for b in range(0, span, QB):
-            part = jnp.full((8, lanes), -jnp.inf, f32)
-            for c in range(b, b + QB, KC):
-                part = jnp.maximum(part, fold8(masked(c), jnp.max))
-            top = jnp.maximum(top, jnp.where(is_far(b), -jnp.inf, part))
-        m = jnp.max(top, axis=0, keepdims=True)
+        border = (far_tiles - tile) * QB
+        tops = []
+        for lo, hi in ((0, border), (border, span)):
+            top = jnp.full((8, lanes), -jnp.inf, f32)
+            for c in range(lo, hi, KC):
+                top = jnp.maximum(top, fold8(masked(c), jnp.max))
+            tops.append(jnp.max(top, axis=0, keepdims=True))
+        m = jnp.maximum(tops[1], jnp.where(first, -jnp.inf, tops[0]))
+        far_m = jnp.where(first, BIG, m)
         total = jnp.zeros((8, lanes), f32)
         dots = jnp.zeros((8, lanes), f32)
         for c in range(0, span, KC):
-            shift = jnp.where(is_far(c), BIG, m)
-            p = jnp.exp2(masked(c) - shift)
+            p = jnp.exp2(masked(c) - (far_m if c < border else m))
             total = total + fold8(p, jnp.sum)
             dots = dots + fold8(p * dpref[c:c + KC, :], jnp.sum)
             sref[c:c + KC, :] = p
@@ -189,26 +167,48 @@
             dshi[c:c + KC, :] = hi
             dslo[c:c + KC, :] = lo
 
-    for n in range(2):
-        tile = 2 * u + n
-        products(tile - 1, sets[1 - n])
-        weights(tile, sets[n])
-
-    @pl.when(u == steps - 1)
-    def _():
-        products(2 * u + 1, sets[1])
-        for n, ref in enumerate(grads):
-            base = n * half
-            for r in range(0, half, QB):
-                dk = dkacc[pl.ds(base + r, QB), :]
-                dv = dvacc[pl.ds(base + r, QB), :]
-                dk = (dk[:, :HD] + dk[:, HD:]) * (1.0 / LOG2E)
-                dv = dv[:, :HD] + dv[:, HD:]
-                if n < carried - 1:
-                    dk = dk + given[n][pl.ds(r, QB), :HD]
-                    dv = dv + given[n][pl.ds(r, QB), HD:]
-                ref[pl.ds(r, QB), :HD] = dk
-                ref[pl.ds(r, QB), HD:] = dv
+    def products(tile):
+        phi, plo, dshi, dslo = sets[tile % 2][2:]
+        a = tile * QB
+        q2 = qall[tile]
+        o2 = oall[tile]
+        pieces = [(c, PC) for c in range(0, tokens, PC)] + [(tokens, QB)]
+        for acc, high, low, rhs in ((dvacc, phi, plo, o2), (dkacc, dshi, dslo, q2)):
+            for c, n in pieces:
+                value = dot(high[c:c + n, :], rhs) + dot(low[c:c + n, :], rhs)
+                if tile and c < tokens:
+                    acc[a + c:a + c + n, :] += value
+                else:
+                    acc[a + c:a + c + n, :] = value
+        kts = kt[:, a:a + span]
+        both = dot(kts, dshi[...]) + dot(kts, dslo[...])
+        dqt = (both[:HD] + both[HD:]) * score_scale
+        for h in range(group):
+            dq_ref[done_rows + a:done_rows + a + QB, h * HD:(h + 1) * HD] = (
+                dqt[:, h * QB:(h + 1) * QB].T)
+
+    def finish(r):
+        n, row = r // half, r % half
+        dk = dkacc[r:r + QB, :]
+        dv = dvacc[r:r + QB, :]
+        dk = (dk[:, :HD] + dk[:, HD:]) * (1.0 / LOG2E)
+        dv = dv[:, :HD] + dv[:, HD:]
+        if n < carried - 1:
+            dk = dk + given[n][row:row + QB, :HD]
+            dv = dv + given[n][row:row + QB, HD:]
+        grads[n][row:row + QB, :HD] = dk
+        grads[n][row:row + QB, HD:] = dv
+
+    scores(0)
+    for tile in range(count):
+        if tile + 1 < count:
+            scores(tile + 1)
+        if tile:
+            products(tile - 1)
+        softmax(tile)
+    products(count - 1)
+    for r in range(0, tokens + half, QB):
+        finish(r)
 
 
 def attn(place, blocks, part, far, own, given, group):
@@ -217,40 +217,35 @@
     lanes = group * QB
     tiles = half // QB
     assert blocks[0].shape[0] == QB
-    whole = pl.BlockSpec((half, 2 * HD), lambda t, s: (0, 0))
-    pick = [pl.BlockSpec(x.shape, lambda t, s, n=x.ndim: (0,) * n) for x in (*own, *far)]
-    buf = [pltpu.VMEM((span, lanes), bf16)] * 4 + [pltpu.VMEM((lanes, 2 * HD), bf16)] * 2
+    vmem = pl.BlockSpec(memory_space=pltpu.VMEM)
     dq_shape = ((1 + part) * half, group * HD)
+    buf = (
+        [pltpu.VMEM((span, lanes), f32)] * 2
+        + [pltpu.VMEM((span, lanes), bf16)] * 4
+    )
+    operands = (*blocks, *own, *far, *given)
     return pl.pallas_call(
         functools.partial(attn_kernel, group, part, len(blocks), len(given)),
-        grid_spec=pltpu.PrefetchScalarGridSpec(
-            num_scalar_prefetch=1,
-            grid=(tiles // 2,),
-            in_specs=[
-                *[pl.BlockSpec(x.shape, lambda t, s: (0, 0)) for x in blocks],
-                *pick, *[pl.BlockSpec(x.shape, lambda t, s: (0, 0)) for x in given],
-            ],
-            out_specs=[pl.BlockSpec(dq_shape, lambda t, s: (0, 0)), whole, whole, whole],
-            scratch_shapes=[
-                pltpu.VMEM((3 * half, 2 * HD), bf16),
-                pltpu.VMEM((3 * half, 2 * HD), bf16),
-                pltpu.VMEM((2 * HD, 3 * half), bf16),
-                pltpu.VMEM((3 * half, 2 * HD), f32),
-                pltpu.VMEM((3 * half, 2 * HD), f32),
-                pltpu.VMEM((span, lanes), f32),
-                pltpu.VMEM((span, lanes), f32),
-                *buf,
-                *buf,
-                pltpu.VMEM((tiles, *blocks[0].shape), f32),
-            ],
-        ),
+        in_specs=[pl.BlockSpec(memory_space=pltpu.SMEM)] + [vmem] * len(operands),
+        out_specs=[vmem] * 4,
+        scratch_shapes=[
+            pltpu.VMEM((3 * half, 2 * HD), bf16),
+            pltpu.VMEM((3 * half, 2 * HD), bf16),
+            pltpu.VMEM((2 * HD, 3 * half), bf16),
+            pltpu.VMEM((3 * half, 2 * HD), f32),
+            pltpu.VMEM((3 * half, 2 * HD), f32),
+            pltpu.VMEM((tiles, *blocks[0].shape), f32),
+            pltpu.VMEM((tiles, lanes, 2 * HD), bf16),
+            pltpu.VMEM((tiles, lanes, 2 * HD), bf16),
+            *buf,
+            *buf,
+        ],
         out_shape=[
             jax.ShapeDtypeStruct(dq_shape, f32),
             *[jax.ShapeDtypeStruct((half, 2 * HD), f32)] * 3,
         ],
-        compiler_params=pltpu.CompilerParams(
-            dimension_semantics=("arbitrary",), vmem_limit_bytes=ATTN_VMEM),
-    )(place, *blocks, *own, *far, *given)
+        compiler_params=pltpu.CompilerParams(vmem_limit_bytes=ATTN_VMEM),
+    )(place, *operands)
 
 
 def spread_kernel(parts, place_ref, *refs):

time: 134 us -> 130 us (0.970)
  Pallas kernels: 29.3 us -> 25 us
    pallas_call x2, Pallas kernels: 23.4 us -> 19.2 us  [attn(): pl.pallas_call(functools.partial(attn_kernel, group, part, len(blocks), l...]
where the time goes in v1:
time: 130 us; the launch traced here: 129 us
  starting transfers between devices  62.2 us (48%)
  waiting for transfers between devices  38.6 us (30%)
  Pallas kernels  25 us (19%)
  local copies, waits for them, and re-layouts  2.16 us (2%)
    ppermute x28, starting transfers between devices, exchanged(): return lax.ppermute(x, ('head', 'inner'), pairs)  47.8 us
    ppermute x28, waiting for transfers between devices, exchanged(): return lax.ppermute(x, ('head', 'inner'), pairs)  28.2 us
    pallas_call x2, Pallas kernels, attn(): pl.pallas_call(functools.partial(attn_kernel, group, part, len(blocks), l...  19.2 us
    ppermute x4, waiting for transfers between devices, shifted(): lax.ppermute(x, 'outer', [(i, i + by) for i in range(devices) if 0 <= i +...  10.4 us
    ppermute x4, starting transfers between devices, shifted(): lax.ppermute(x, 'outer', [(i, i + by) for i in range(devices) if 0 <= i +...  9.98 us
    all_to_all x1, starting transfers between devices, swap(): return lax.all_to_all(x, PLANE, split_axis=0, concat_axis=0, tiled=True)  4.42 us
  transfers between devices with their start and end apart: 33, of which 10 were waited for; matrix products, arithmetic and copies ran while one was open for 0% of the time, Pallas kernels for 3%

profile of v1, /device:TPU:0, one launch (start us, length us, event | category | flops | bytes accessed | tf_op | source)
XLA Modules:
  0.0 129.1 jit_solution(4915973763743839670)
XLA Ops:
  3.7 3.0 %collective-permute-start.8 = (f32[128,256]{1,0:T(8,128)S(1)}, f32[128,256]{1,0:T(8,128)S(1)}, u32[]{:S(2)}, u32[]{:S(2)}) collective-permute-start(f32[128,256]{1,0:T(8,128)S(1)} %get-tuple-element.47), channel_id=1, source_target_pairs={{0,16},{1,17},{8,24},{9,25},{16,0},{17,1},{24,8},{25,9},{2,18},{3,... | collective-permute-start | bytes 393224 | tf_op jit(solution)/shard_map/ppermute | solution.py:370
  8.5 2.7 %collective-permute-start.12 = (f32[128,256]{1,0:T(8,128)S(1)}, f32[128,256]{1,0:T(8,128)S(1)}, u32[]{:S(2)}, u32[]{:S(2)}) collective-permute-start(f32[128,256]{1,0:T(8,128)S(1)} %get-tuple-element.51), channel_id=1, source_target_pairs={{0,17},{1,16},{8,25},{9,24},{16,1},{17,0},{24,9},{25,8},{2,19},{3,... | collective-permute-start | bytes 393224 | tf_op jit(solution)/shard_map/ppermute | solution.py:370
  11.5 1.9 %collective-permute-done.9.refs_11_ = f32[128,256]{1,0:T(8,128)S(1)} collective-permute-done((f32[128,256]{1,0:T(8,128)S(1)}, f32[128,256]{1,0:T(8,128)S(1)}, u32[]{:S(2)}, u32[]{:S(2)}) %collective-permute-start.9) | collective-permute-done | bytes 131104 | tf_op jit(solution)/shard_map/ppermute | solution.py:370
  13.5 7.0 %collective-permute-done.11.refs_13_ = f32[128,256]{1,0:T(8,128)S(1)} collective-permute-done((f32[128,256]{1,0:T(8,128)S(1)}, f32[128,256]{1,0:T(8,128)S(1)}, u32[]{:S(2)}, u32[]{:S(2)}) %collective-permute-start.11) | collective-permute-done | bytes 131104 | tf_op jit(solution)/shard_map/ppermute | solution.py:370
  20.5 4.0 %collective-permute-start.15 = (f32[6,128,256]{2,1,0:T(8,128)S(1)}, f32[6,128,256]{2,1,0:T(8,128)S(1)}, u32[]{:S(2)}, u32[]{:S(2)}) collective-permute-start(f32[6,128,256]{2,1,0:T(8,128)S(1)} %bitcast_dynamic-update-slice_fusion), channel_id=1, source_target_pairs={{0,2},{2,4},{4,6},{1,3},{3,5},{5,7},{8,10},{10,12},{12,14},{9,11},... | collective-permute-start | bytes 2359304 | tf_op jit(solution)/shard_map/ppermute | solution.py:359
  26.2 1.8 %collective-permute-start.1 = (f32[128,512]{1,0:T(8,128)S(1)}, f32[128,512]{1,0:T(8,128)S(1)}, u32[]{:S(2)}, u32[]{:S(2)}) collective-permute-start(f32[128,512]{1,0:T(8,128)S(1)} %get-tuple-element.39), channel_id=1, source_target_pairs={{0,16},{1,17},{8,24},{9,25},{16,0},{17,1},{24,8},{25,9},{2,18},{3,... | collective-permute-start | bytes 786440 | tf_op jit(solution)/shard_map/ppermute | solution.py:370
  29.8 5.6 %collective-permute-done.1.refs_2_ = f32[128,512]{1,0:T(8,128)S(1)} collective-permute-done((f32[128,512]{1,0:T(8,128)S(1)}, f32[128,512]{1,0:T(8,128)S(1)}, u32[]{:S(2)}, u32[]{:S(2)}) %collective-permute-start.1) | collective-permute-done | bytes 262176 | tf_op jit(solution)/shard_map/ppermute | solution.py:370
  35.4 2.8 %collective-permute-start.5 = (f32[128,512]{1,0:T(8,128)S(1)}, f32[128,512]{1,0:T(8,128)S(1)}, u32[]{:S(2)}, u32[]{:S(2)}) collective-permute-start(f32[128,512]{1,0:T(8,128)S(1)} %get-tuple-element.43), channel_id=1, source_target_pairs={{0,17},{1,16},{8,25},{9,24},{16,1},{17,0},{24,9},{25,8},{2,19},{3,... | collective-permute-start | bytes 786440 | tf_op jit(solution)/shard_map/ppermute | solution.py:370
  38.1 2.2 %collective-permute-done.2.refs_3_ = f32[128,512]{1,0:T(8,128)S(1)} collective-permute-done((f32[128,512]{1,0:T(8,128)S(1)}, f32[128,512]{1,0:T(8,128)S(1)}, u32[]{:S(2)}, u32[]{:S(2)}) %collective-permute-start.2) | collective-permute-done | bytes 262176 | tf_op jit(solution)/shard_map/ppermute | solution.py:370
  40.3 3.2 %collective-permute-start.6 = (f32[128,512]{1,0:T(8,128)S(1)}, f32[128,512]{1,0:T(8,128)S(1)}, u32[]{:S(2)}, u32[]{:S(2)}) collective-permute-start(f32[128,512]{1,0:T(8,128)S(1)} %get-tuple-element.44), channel_id=1, source_target_pairs={{0,25},{1,24},{8,17},{9,16},{16,9},{17,8},{24,1},{25,0},{2,27},{3,... | collective-permute-start | bytes 786440 | tf_op jit(solution)/shard_map/ppermute | solution.py:370
  43.5 3.4 %collective-permute-start.14 = (f32[2,128,256]{2,1,0:T(8,128)S(1)}, f32[2,128,256]{2,1,0:T(8,128)S(1)}, u32[]{:S(2)}, u32[]{:S(2)}) collective-permute-start(f32[2,128,256]{2,1,0:T(8,128)S(1)} %pad_maximum_fusion), channel_id=1, source_target_pairs={{0,2},{2,4},{4,6},{1,3},{3,5},{5,7},{8,10},{10,12},{12,14},{9,11},... | collective-permute-start | bytes 786440 | tf_op jit(solution)/shard_map/ppermute | solution.py:359
  46.9 5.9 %collective-permute-done.4.refs_5_ = f32[128,512]{1,0:T(8,128)S(1)} collective-permute-done((f32[128,512]{1,0:T(8,128)S(1)}, f32[128,512]{1,0:T(8,128)S(1)}, u32[]{:S(2)}, u32[]{:S(2)}) %collective-permute-start.4) | collective-permute-done | bytes 262176 | tf_op jit(solution)/shard_map/ppermute | solution.py:370
  52.8 9.0 %shard_map.69 = (f32[512,256]{1,0:T(8,128)S(1)}, f32[512,256]{1,0:T(8,128)S(1)}, f32[512,256]{1,0:T(8,128)S(1)}, f32[512,256]{1,0:T(8,128)S(1)}) custom-call(s32[2]{0:T(128)S(1)} %pad_add_fusion.place_ref, f32[128,512]{1,0:T(8,128)S(1)} %get-tuple-element.37.refs_0_, f32[128,512]{1,0:T(8,128)S(1)} %collective-permute-done.refs_1_, ...), custom_call_target="tpu_custom_call" | custom-call | tf_op jit(solution)/shard_map/pallas_call | solution.py:227
  61.9 10.1 %shard_map.70 = (f32[1024,256]{1,0:T(8,128)}, f32[512,256]{1,0:T(8,128)}, f32[512,256]{1,0:T(8,128)S(1)}, f32[512,256]{1,0:T(8,128)S(1)}) custom-call(s32[2]{0:T(128)S(1)} %pad_add_fusion.place_ref, f32[128,512]{1,0:T(8,128)S(1)} %get-tuple-element.37.refs_0_, f32[128,512]{1,0:T(8,128)S(1)} %collective-permute-done.refs_1_, ...), custom_call_target="tpu_custom_call" | custom-call | tf_op jit(solution)/shard_map/pallas_call | solution.py:227
  73.3 4.4 %all-to-all-start = ((f32[8,128,256]{2,1,0:T(8,128)}), f32[8,128,256]{2,1,0:T(8,128)S(1)}, u32[]{:S(2)}, u32[]{:S(2)}) async-start(f32[8,128,256]{2,1,0:T(8,128)} %bitcast.10), calls=%async_computation | async-start | bytes 2097152 | tf_op jit(solution)/shard_map/all_to_all | solution.py:354
  79.0 9.9 %collective-permute-done.24.back_ref = f32[512,256]{1,0:T(8,128)S(1)} collective-permute-done((f32[512,256]{1,0:T(8,128)}, f32[512,256]{1,0:T(8,128)S(1)}, u32[]{:S(2)}, u32[]{:S(2)}) %collective-permute-start.24) | collective-permute-done | bytes 524320 | tf_op jit(solution)/shard_map/ppermute | solution.py:359
  89.5 3.4 %collective-permute-start.28 = (f32[128,256]{1,0:T(8,128)S(1)}, f32[128,256]{1,0:T(8,128)S(1)}, u32[]{:S(2)}, u32[]{:S(2)}) collective-permute-start(f32[128,256]{1,0:T(8,128)S(1)} %get-tuple-element.65.refs_8_), channel_id=1, source_target_pairs={{0,1},{8,9},{16,17},{24,25},{2,3},{10,11},{18,19},{26,27},{4,5},{1... | collective-permute-start | bytes 393224 | tf_op jit(solution)/shard_map/ppermute | solution.py:370
  94.9 4.1 %collective-permute-start.30 = (f32[128,256]{1,0:T(8,128)S(1)}, f32[128,256]{1,0:T(8,128)S(1)}, u32[]{:S(2)}, u32[]{:S(2)}) collective-permute-start(f32[128,256]{1,0:T(8,128)S(1)} %get-tuple-element.67), channel_id=1, source_target_pairs={{0,17},{8,25},{16,1},{24,9},{2,19},{10,27},{18,3},{26,11},{4,21},{... | collective-permute-start | bytes 393224 | tf_op jit(solution)/shard_map/ppermute | solution.py:370
  100.9 5.0 %collective-permute-start.31 = (f32[128,256]{1,0:T(8,128)S(1)}, f32[128,256]{1,0:T(8,128)S(1)}, u32[]{:S(2)}, u32[]{:S(2)}) collective-permute-start(f32[128,256]{1,0:T(8,128)S(1)} %get-tuple-element.68), channel_id=1, source_target_pairs={{0,25},{8,17},{16,9},{24,1},{2,27},{10,19},{18,11},{26,3},{4,29},{... | collective-permute-start | bytes 393224 | tf_op jit(solution)/shard_map/ppermute | solution.py:370
  109.3 3.1 %collective-permute-start.17 = (f32[128,256]{1,0:T(8,128)S(1)}, f32[128,256]{1,0:T(8,128)S(1)}, u32[]{:S(2)}, u32[]{:S(2)}) collective-permute-start(f32[128,256]{1,0:T(8,128)S(1)} %get-tuple-element.60), channel_id=1, source_target_pairs={{0,8},{8,0},{16,24},{24,16},{2,10},{10,2},{18,26},{26,18},{4,12},{... | collective-permute-start | bytes 393224 | tf_op jit(solution)/shard_map/ppermute | solution.py:370
  113.7 3.8 %collective-permute-start.18 = (f32[128,256]{1,0:T(8,128)S(1)}, f32[128,256]{1,0:T(8,128)S(1)}, u32[]{:S(2)}, u32[]{:S(2)}) collective-permute-start(f32[128,256]{1,0:T(8,128)S(1)} %get-tuple-element.61), channel_id=1, source_target_pairs={{0,16},{8,24},{16,0},{24,8},{2,18},{10,26},{18,2},{26,10},{4,20},{... | collective-permute-start | bytes 393224 | tf_op jit(solution)/shard_map/ppermute | solution.py:370
  118.8 1.9 %collective-permute-start.19 = (f32[128,256]{1,0:T(8,128)S(1)}, f32[128,256]{1,0:T(8,128)S(1)}, u32[]{:S(2)}, u32[]{:S(2)}) collective-permute-start(f32[128,256]{1,0:T(8,128)S(1)} %get-tuple-element.62), channel_id=1, source_target_pairs={{0,24},{8,16},{16,8},{24,0},{2,26},{10,18},{18,10},{26,2},{4,28},{... | collective-permute-start | bytes 393224 | tf_op jit(solution)/shard_map/ppermute | solution.py:370
  121.1 4.9 %collective-permute-done.23.refs_7_ = f32[128,256]{1,0:T(8,128)S(1)} collective-permute-done((f32[128,256]{1,0:T(8,128)S(1)}, f32[128,256]{1,0:T(8,128)S(1)}, u32[]{:S(2)}, u32[]{:S(2)}) %collective-permute-start.23) | collective-permute-done | bytes 131104 | tf_op jit(solution)/shard_map/ppermute | solution.py:370
  126.4 1.6 %unpack_kv.1 = (f32[128,1024]{1,0:T(8,128)}, f32[128,1024]{1,0:T(8,128)}) custom-call(s32[2]{0:T(128)S(1)} %pad_add_fusion.place_ref, f32[128,256]{1,0:T(8,128)S(1)} %get-tuple-element.59.refs_0_, f32[128,256]{1,0:T(8,128)S(1)} %collective-permute-done.17.refs_1_, f32[128,256]{1,0:T(8,128)S(1)} %collective-permute-done.18.refs_2_, ...), custom_call_target="tpu_custom_call" | custom-call | tf_op jit(solution)/shard_map/unpack_kv/pallas_call | solution.py:340
  (66 shorter events, 23.3 us)
Async XLA Ops:
  8.3 12.2 %collective-permute-start.11 = (f32[128,256]{1,0:T(8,128)S(1)}, f32[128,256]{1,0:T(8,128)S(1)}, u32[]{:S(2)}, u32[]{:S(2)}) collective-permute-start(f32[128,256]{1,0:T(8,128)S(1)} %get-tuple-element.50), channel_id=1, source_target_pairs={{0,9},{1,8},{8,1},{9,0},{16,25},{17,24},{24,17},{25,16},{2,11},{3,... | collective-permute-start | bytes 393224 | tf_op jit(solution)/shard_map/ppermute | solution.py:370
  8.5 11.9 %collective-permute-start.12 = (f32[128,256]{1,0:T(8,128)S(1)}, f32[128,256]{1,0:T(8,128)S(1)}, u32[]{:S(2)}, u32[]{:S(2)}) collective-permute-start(f32[128,256]{1,0:T(8,128)S(1)} %get-tuple-element.51), channel_id=1, source_target_pairs={{0,17},{1,16},{8,25},{9,24},{16,1},{17,0},{24,9},{25,8},{2,19},{3,... | collective-permute-start | bytes 393224 | tf_op jit(solution)/shard_map/ppermute | solution.py:370
  11.2 9.3 %collective-permute-start.13 = (f32[128,256]{1,0:T(8,128)S(1)}, f32[128,256]{1,0:T(8,128)S(1)}, u32[]{:S(2)}, u32[]{:S(2)}) collective-permute-start(f32[128,256]{1,0:T(8,128)S(1)} %get-tuple-element.52), channel_id=1, source_target_pairs={{0,25},{1,24},{8,17},{9,16},{16,9},{17,8},{24,1},{25,0},{2,27},{3,... | collective-permute-start | bytes 393224 | tf_op jit(solution)/shard_map/ppermute | solution.py:370
  20.5 32.3 %collective-permute-start.15 = (f32[6,128,256]{2,1,0:T(8,128)S(1)}, f32[6,128,256]{2,1,0:T(8,128)S(1)}, u32[]{:S(2)}, u32[]{:S(2)}) collective-permute-start(f32[6,128,256]{2,1,0:T(8,128)S(1)} %bitcast_dynamic-update-slice_fusion), channel_id=1, source_target_pairs={{0,2},{2,4},{4,6},{1,3},{3,5},{5,7},{8,10},{10,12},{12,14},{9,11},... | collective-permute-start | bytes 2359304 | tf_op jit(solution)/shard_map/ppermute | solution.py:359
  26.2 9.2 %collective-permute-start.1 = (f32[128,512]{1,0:T(8,128)S(1)}, f32[128,512]{1,0:T(8,128)S(1)}, u32[]{:S(2)}, u32[]{:S(2)}) collective-permute-start(f32[128,512]{1,0:T(8,128)S(1)} %get-tuple-element.39), channel_id=1, source_target_pairs={{0,16},{1,17},{8,24},{9,25},{16,0},{17,1},{24,8},{25,9},{2,18},{3,... | collective-permute-start | bytes 786440 | tf_op jit(solution)/shard_map/ppermute | solution.py:370
  28.0 12.3 %collective-permute-start.2 = (f32[128,512]{1,0:T(8,128)S(1)}, f32[128,512]{1,0:T(8,128)S(1)}, u32[]{:S(2)}, u32[]{:S(2)}) collective-permute-start(f32[128,512]{1,0:T(8,128)S(1)} %get-tuple-element.40), channel_id=1, source_target_pairs={{0,24},{1,25},{8,16},{9,17},{16,8},{17,9},{24,0},{25,1},{2,26},{3,... | collective-permute-start | bytes 786440 | tf_op jit(solution)/shard_map/ppermute | solution.py:370
  28.0 15.5 %collective-permute-start.3 = (f32[128,512]{1,0:T(8,128)S(1)}, f32[128,512]{1,0:T(8,128)S(1)}, u32[]{:S(2)}, u32[]{:S(2)}) collective-permute-start(f32[128,512]{1,0:T(8,128)S(1)} %get-tuple-element.41), channel_id=1, source_target_pairs={{0,1},{1,0},{8,9},{9,8},{16,17},{17,16},{24,25},{25,24},{2,3},{3,2... | collective-permute-start | bytes 786440 | tf_op jit(solution)/shard_map/ppermute | solution.py:370
  29.6 23.2 %collective-permute-start.4 = (f32[128,512]{1,0:T(8,128)S(1)}, f32[128,512]{1,0:T(8,128)S(1)}, u32[]{:S(2)}, u32[]{:S(2)}) collective-permute-start(f32[128,512]{1,0:T(8,128)S(1)} %get-tuple-element.42), channel_id=1, source_target_pairs={{0,9},{1,8},{8,1},{9,0},{16,25},{17,24},{24,17},{25,16},{2,11},{3,... | collective-permute-start | bytes 786440 | tf_op jit(solution)/shard_map/ppermute | solution.py:370
  35.4 17.4 %collective-permute-start.5 = (f32[128,512]{1,0:T(8,128)S(1)}, f32[128,512]{1,0:T(8,128)S(1)}, u32[]{:S(2)}, u32[]{:S(2)}) collective-permute-start(f32[128,512]{1,0:T(8,128)S(1)} %get-tuple-element.43), channel_id=1, source_target_pairs={{0,17},{1,16},{8,25},{9,24},{16,1},{17,0},{24,9},{25,8},{2,19},{3,... | collective-permute-start | bytes 786440 | tf_op jit(solution)/shard_map/ppermute | solution.py:370
  40.3 12.5 %collective-permute-start.6 = (f32[128,512]{1,0:T(8,128)S(1)}, f32[128,512]{1,0:T(8,128)S(1)}, u32[]{:S(2)}, u32[]{:S(2)}) collective-permute-start(f32[128,512]{1,0:T(8,128)S(1)} %get-tuple-element.44), channel_id=1, source_target_pairs={{0,25},{1,24},{8,17},{9,16},{16,9},{17,8},{24,1},{25,0},{2,27},{3,... | collective-permute-start | bytes 786440 | tf_op jit(solution)/shard_map/ppermute | solution.py:370
  43.5 9.3 %collective-permute-start.14 = (f32[2,128,256]{2,1,0:T(8,128)S(1)}, f32[2,128,256]{2,1,0:T(8,128)S(1)}, u32[]{:S(2)}, u32[]{:S(2)}) collective-permute-start(f32[2,128,256]{2,1,0:T(8,128)S(1)} %pad_maximum_fusion), channel_id=1, source_target_pairs={{0,2},{2,4},{4,6},{1,3},{3,5},{5,7},{8,10},{10,12},{12,14},{9,11},... | collective-permute-start | bytes 786440 | tf_op jit(solution)/shard_map/ppermute | solution.py:359
  72.0 16.9 %collective-permute-start.24 = (f32[512,256]{1,0:T(8,128)}, f32[512,256]{1,0:T(8,128)S(1)}, u32[]{:S(2)}, u32[]{:S(2)}) collective-permute-start(f32[512,256]{1,0:T(8,128)} %get-tuple-element.64), channel_id=1, source_target_pairs={{2,0},{4,2},{6,4},{3,1},{5,3},{7,5},{10,8},{12,10},{14,12},{11,9},... | collective-permute-start | bytes 1572872 | tf_op jit(solution)/shard_map/ppermute | solution.py:359
  73.3 54.8 %all-to-all-start = ((f32[8,128,256]{2,1,0:T(8,128)}), f32[8,128,256]{2,1,0:T(8,128)S(1)}, u32[]{:S(2)}, u32[]{:S(2)}) async-start(f32[8,128,256]{2,1,0:T(8,128)} %bitcast.10), calls=%async_computation | async-start | bytes 2097152 | tf_op jit(solution)/shard_map/all_to_all | solution.py:354
  77.7 21.9 %collective-permute-start.16 = (f32[512,256]{1,0:T(8,128)S(1)}, f32[512,256]{1,0:T(8,128)S(1)}, u32[]{:S(2)}, u32[]{:S(2)}) collective-permute-start(f32[512,256]{1,0:T(8,128)S(1)} %get-tuple-element.58), channel_id=1, source_target_pairs={{2,0},{4,2},{6,4},{3,1},{5,3},{7,5},{10,8},{12,10},{14,12},{11,9},... | collective-permute-start | bytes 1572872 | tf_op jit(solution)/shard_map/ppermute | solution.py:359
  89.5 11.4 %collective-permute-start.28 = (f32[128,256]{1,0:T(8,128)S(1)}, f32[128,256]{1,0:T(8,128)S(1)}, u32[]{:S(2)}, u32[]{:S(2)}) collective-permute-start(f32[128,256]{1,0:T(8,128)S(1)} %get-tuple-element.65.refs_8_), channel_id=1, source_target_pairs={{0,1},{8,9},{16,17},{24,25},{2,3},{10,11},{18,19},{26,27},{4,5},{1... | collective-permute-start | bytes 393224 | tf_op jit(solution)/shard_map/ppermute | solution.py:370
  92.9 13.0 %collective-permute-start.29 = (f32[128,256]{1,0:T(8,128)S(1)}, f32[128,256]{1,0:T(8,128)S(1)}, u32[]{:S(2)}, u32[]{:S(2)}) collective-permute-start(f32[128,256]{1,0:T(8,128)S(1)} %get-tuple-element.66), channel_id=1, source_target_pairs={{0,9},{8,1},{16,25},{24,17},{2,11},{10,3},{18,27},{26,19},{4,13},{... | collective-permute-start | bytes 393224 | tf_op jit(solution)/shard_map/ppermute | solution.py:370
  94.2 12.4 %collective-permute-start.25 = (f32[128,256]{1,0:T(8,128)S(1)}, f32[128,256]{1,0:T(8,128)S(1)}, u32[]{:S(2)}, u32[]{:S(2)}) collective-permute-start(f32[128,256]{1,0:T(8,128)S(1)} %get-tuple-element.66), channel_id=1, source_target_pairs={{1,9},{9,1},{17,25},{25,17},{3,11},{11,3},{19,27},{27,19},{5,13},{... | collective-permute-start | bytes 393224 | tf_op jit(solution)/shard_map/ppermute | solution.py:370
  94.9 13.0 %collective-permute-start.30 = (f32[128,256]{1,0:T(8,128)S(1)}, f32[128,256]{1,0:T(8,128)S(1)}, u32[]{:S(2)}, u32[]{:S(2)}) collective-permute-start(f32[128,256]{1,0:T(8,128)S(1)} %get-tuple-element.67), channel_id=1, source_target_pairs={{0,17},{8,25},{16,1},{24,9},{2,19},{10,27},{18,3},{26,11},{4,21},{... | collective-permute-start | bytes 393224 | tf_op jit(solution)/shard_map/ppermute | solution.py:370
  99.6 9.7 %collective-permute-start.26 = (f32[128,256]{1,0:T(8,128)S(1)}, f32[128,256]{1,0:T(8,128)S(1)}, u32[]{:S(2)}, u32[]{:S(2)}) collective-permute-start(f32[128,256]{1,0:T(8,128)S(1)} %get-tuple-element.67), channel_id=1, source_target_pairs={{1,17},{9,25},{17,1},{25,9},{3,19},{11,27},{19,3},{27,11},{5,21},{... | collective-permute-start | bytes 393224 | tf_op jit(solution)/shard_map/ppermute | solution.py:370
  100.9 11.5 %collective-permute-start.31 = (f32[128,256]{1,0:T(8,128)S(1)}, f32[128,256]{1,0:T(8,128)S(1)}, u32[]{:S(2)}, u32[]{:S(2)}) collective-permute-start(f32[128,256]{1,0:T(8,128)S(1)} %get-tuple-element.68), channel_id=1, source_target_pairs={{0,25},{8,17},{16,9},{24,1},{2,27},{10,19},{18,11},{26,3},{4,29},{... | collective-permute-start | bytes 393224 | tf_op jit(solution)/shard_map/ppermute | solution.py:370
  106.6 10.8 %collective-permute-start.20 = (f32[128,256]{1,0:T(8,128)S(1)}, f32[128,256]{1,0:T(8,128)S(1)}, u32[]{:S(2)}, u32[]{:S(2)}) collective-permute-start(f32[128,256]{1,0:T(8,128)S(1)} %get-tuple-element.59.refs_0_), channel_id=1, source_target_pairs={{1,0},{9,8},{17,16},{25,24},{3,2},{11,10},{19,18},{27,26},{5,4},{1... | collective-permute-start | bytes 393224 | tf_op jit(solution)/shard_map/ppermute | solution.py:370
  107.9 10.8 %collective-permute-start.21 = (f32[128,256]{1,0:T(8,128)S(1)}, f32[128,256]{1,0:T(8,128)S(1)}, u32[]{:S(2)}, u32[]{:S(2)}) collective-permute-start(f32[128,256]{1,0:T(8,128)S(1)} %get-tuple-element.60), channel_id=1, source_target_pairs={{1,8},{9,0},{17,24},{25,16},{3,10},{11,2},{19,26},{27,18},{5,12},{... | collective-permute-start | bytes 393224 | tf_op jit(solution)/shard_map/ppermute | solution.py:370
  109.3 11.5 %collective-permute-start.17 = (f32[128,256]{1,0:T(8,128)S(1)}, f32[128,256]{1,0:T(8,128)S(1)}, u32[]{:S(2)}, u32[]{:S(2)}) collective-permute-start(f32[128,256]{1,0:T(8,128)S(1)} %get-tuple-element.60), channel_id=1, source_target_pairs={{0,8},{8,0},{16,24},{24,16},{2,10},{10,2},{18,26},{26,18},{4,12},{... | collective-permute-start | bytes 393224 | tf_op jit(solution)/shard_map/ppermute | solution.py:370
  117.5 8.5 %collective-permute-start.23 = (f32[128,256]{1,0:T(8,128)S(1)}, f32[128,256]{1,0:T(8,128)S(1)}, u32[]{:S(2)}, u32[]{:S(2)}) collective-permute-start(f32[128,256]{1,0:T(8,128)S(1)} %get-tuple-element.62), channel_id=1, source_target_pairs={{1,24},{9,16},{17,8},{25,0},{3,26},{11,18},{19,10},{27,2},{5,28},{... | collective-permute-start | bytes 393224 | tf_op jit(solution)/shard_map/ppermute | solution.py:370
  (13 other events, 104.2 us)
